TPU v7x, 32 devices: a whole 2x2x4 slice. The times are simulated.
32 devices in a mesh: dp: 8 (over z, y), mp: 4 (over x, core).
Axes of the slice: x: 2, y: 2, z: 4, core: 2. Of those that a mesh axis runs over, the one named last changes fastest.
Arguments:
- hidden: bfloat16 [5632, 7168], P('dp', 'mp'), may hold values from -0.1875 to 0.1875
- router_weight: bfloat16 [7168, 256], P(('mp', 'dp')), may hold values from -3 to 3
- logits: float32 [5632, 256], P(('dp', 'mp')), may hold values from -12 to 240
- first_pot: float32 [256], replicated, may hold values from -1 to 1
- second_pot: float32 [256], replicated, may hold values from -1 to 1
- expert_index: int32 [5632], P(('dp', 'mp')), may hold values from 0 to 255
- loss_grad: float32 [5632], P(('dp', 'mp')), may hold values from -9 to 9
Outputs:
- weight_grad: float32 [7168, 256], P(('mp', 'dp'))
- hidden_grad: bfloat16 [5632, 7168], P('dp', 'mp')
All inputs are finite; a program needn't handle non-finite values.
Results may differ from a plain program's by a relative error of at most 0.005.
Values may be sent and summed in bfloat16 or wider, within the bound.
A program may use at most 64 MiB of HBM per device.

v0:
```python
import jax
import jax.numpy as jnp
from jax import lax
from jax.sharding import PartitionSpec as P


def neg_lse(values):
    top = jnp.max(values, axis=1, keepdims=True)
    return -(top[:, 0] + jnp.log(jnp.sum(jnp.exp(values - top), axis=1)))


def body(hidden, router_weight, logits, first_pot, second_pot, expert_index, loss_grad):
    experts = logits.shape[1]
    total_tokens = logits.shape[0] * lax.axis_size("dp") * lax.axis_size("mp")
    ratio = experts / total_tokens
    first_row = neg_lse(logits)
    first_soft = jnp.exp(logits + first_row[:, None])
    shifted = logits + first_pot[None, :]
    second_row = neg_lse(shifted)
    second_soft = jnp.exp(shifted + second_row[:, None])
    first_col = ratio * jnp.exp(logits + first_row[:, None] + first_pot[None, :])
    prob = jnp.exp(logits + second_row[:, None] + second_pot[None, :])
    second_col = ratio * prob
    onehot = (expert_index[:, None] == jnp.arange(experts, dtype=jnp.int32)[None, :]).astype(
        jnp.float32
    )
    direct = onehot * prob * loss_grad[:, None]
    row_direct = jnp.sum(direct, axis=1)
    second_colgrad = lax.psum(jnp.sum(direct, axis=0), ("dp", "mp"))
    second_rowgrad = row_direct - jnp.dot(
        second_col, second_colgrad, precision=lax.Precision.HIGHEST
    )
    first_colgrad = lax.psum(-jnp.sum(second_rowgrad[:, None] * second_soft, axis=0), ("dp", "mp"))
    first_rowgrad = -jnp.dot(first_col, first_colgrad, precision=lax.Precision.HIGHEST)
    score_grad = (
        direct
        - second_colgrad[None, :] * second_col
        - second_rowgrad[:, None] * second_soft
        - first_colgrad[None, :] * first_col
        - first_rowgrad[:, None] * first_soft
    ).astype(jnp.bfloat16)
    score_full = lax.all_gather(score_grad, "mp", axis=0, tiled=True)
    hidden_grad = lax.dot_general(
        score_full,
        lax.all_gather(router_weight, "dp", axis=0, tiled=True),
        (((1,), (1,)), ((), ())),
        preferred_element_type=jnp.float32,
    ).astype(jnp.bfloat16)
    weight_grad = lax.psum_scatter(
        lax.dot_general(
            hidden, score_full, (((0,), (0,)), ((), ())), preferred_element_type=jnp.float32
        ),
        "dp",
        scatter_dimension=0,
        tiled=True,
    )
    return (weight_grad, hidden_grad)


def solution(mesh):
    in_specs = (
        P("dp", "mp"),
        P(("mp", "dp"), None),
        P(("dp", "mp"), None),
        P(),
        P(),
        P(("dp", "mp")),
        P(("dp", "mp")),
    )
    out_specs = (P(("mp", "dp"), None), P("dp", "mp"))
    return jax.shard_map(body, mesh=mesh, in_specs=in_specs, out_specs=out_specs, check_vma=False)
```

profile of v0, /device:TPU:0, one launch (start us, length us, event | category | flops | bytes accessed | tf_op | source)
XLA Modules:
  0.0 188.7 jit_solution(2244073612009030590)
XLA Ops:
  7.2 0.0 copy-start
  7.2 0.0 reduce-scatter.4.cloned.1.call-start
  7.2 1.2 fusion.15
  8.4 1.2 exponential_reduce_fusion
  9.6 1.2 fusion.5
  10.8 42.0 %psum.14 = f32[256]{0:T(256)S(1)} all-reduce(f32[256]{0:T(256)S(1)} %get-tuple-element.6), channel_id=1, replica_groups=mesh['dp'=8,'mp'=4] {'dp','mp'}, use_global_device_ids=true, to_apply=%region_3.0 | all-reduce | flops 256 | bytes 2048 | tf_op jit(solution)/shard_map/psum | solution.py:29
  52.8 1.2 fusion.2
  54.1 0.1 sub.34
  54.1 1.1 fusion.7
  55.2 40.1 %psum.15 = f32[256]{0:T(256)S(1)} all-reduce(f32[256]{0:T(256)S(1)} %neg.22), channel_id=1, replica_groups=mesh['dp'=8,'mp'=4] {'dp','mp'}, use_global_device_ids=true, to_apply=%region_8.0 | all-reduce | flops 256 | bytes 2048 | tf_op jit(solution)/shard_map/psum | solution.py:33
  95.3 1.2 fusion
  96.6 1.2 subtract_convert_fusion
  97.8 7.1 %all_gather.6 = bf16[704,256]{1,0:T(8,128)(2,1)S(1)} all-gather(bf16[176,256]{1,0:T(8,128)(2,1)S(1)} %subtract_convert_fusion), channel_id=1, replica_groups=mesh['dp'=8,'mp'=4] {'mp'}, dimensions={0}, use_global_device_ids=true | all-gather | bytes 450560 | tf_op jit(solution)/shard_map/all_gather | solution.py:42
  104.9 0.0 copy-done
  104.9 2.1 %convolution_bitcast_fusion = f32[1792,256]{0,1:T(8,128)} fusion(bf16[704,256]{1,0:T(8,128)(2,1)S(1)} %all_gather.6, bf16[704,1792]{1,0:T(8,128)(2,1)S(1)} %copy-done), kind=kOutput, calls=%fused_computation.1 | convolution fusion | flops 645922816 | bytes 4718592 | tf_op jit(solution)/shard_map/dot_general | solution.py:50
  107.0 0.0 copy-start.1
  107.0 2.8 %copy.11 = f32[1792,256]{1,0:T(8,128)} copy(f32[1792,256]{0,1:T(8,128)} %convolution_bitcast_fusion) | data formatting | bytes 3670016
  109.8 0.0 reduce-scatter.4.cloned.1.call-update
  109.8 0.0 copy-done.1
  109.8 34.5 %all_gather.7 = bf16[1792,256]{1,0:T(8,128)(2,1)S(1)} all-gather(bf16[224,256]{1,0:T(8,128)(2,1)S(1)} %copy-done.1), channel_id=1, replica_groups=mesh['dp'=8,'mp'=4] {'dp'}, dimensions={0}, use_global_device_ids=true | all-gather | bytes 1032192 | tf_op jit(solution)/shard_map/all_gather | solution.py:45
  144.4 2.3 %convolution_convert_fusion = bf16[704,1792]{1,0:T(8,128)(2,1)} fusion(bf16[704,256]{1,0:T(8,128)(2,1)S(1)} %all_gather.6, bf16[1792,256]{1,0:T(8,128)(2,1)S(1)} %all_gather.7), kind=kOutput, calls=%fused_computation | convolution fusion | flops 647184384 | bytes 3801088 | tf_op jit(solution)/shard_map/dot_general | solution.py:43
  146.7 35.1 %reduce-scatter.4.cloned.1.call-done = f32[224,256]{1,0:T(8,128)} async-done(((f32[1792,256]{1,0:T(8,128)}), f32[224,256]{1,0:T(8,128)}) %reduce-scatter.4.cloned.1.call-update) | async-done | bytes 229392
  (6 shorter events, 0.0 us)
Async XLA Ops:
  7.2 97.7 %copy-start = (bf16[704,1792]{1,0:T(8,128)(2,1)S(1)}, bf16[704,1792]{1,0:T(8,128)(2,1)}, u32[]{:S(2)}) copy-start(bf16[704,1792]{1,0:T(8,128)(2,1)} %param.7) | copy-start | bytes 7569412
  7.2 174.7 %reduce-scatter.4.cloned.1.call-start = ((), (), s32[]{:S(2)}) async-start(), calls=%async_computation.1 | async-start | bytes 2064384
  107.0 2.8 %copy-start.1 = (bf16[224,256]{1,0:T(8,128)(2,1)S(1)}, bf16[224,256]{1,0:T(8,128)(2,1)}, u32[]{:S(2)}) copy-start(bf16[224,256]{1,0:T(8,128)(2,1)} %param.8) | copy-start | bytes 344068
Sparse Core Ops, SparseCore 0:
  110.0 71.8 reduce-scatter.3
where the time goes:
time: 189 us
  blocking collectives  124 us (66%)
  waiting for transfers between devices  35.1 us (19%)
  between operations  14.1 us (7%)
  matrix products  6.93 us (4%)
  other arithmetic  5.94 us (3%)
  local copies, waits for them, and re-layouts  2.81 us (1%)
    psum x1, blocking collectives, body(): second_colgrad = lax.psum(jnp.sum(direct, axis=0), ('dp', 'mp'))  42 us
    psum x1, blocking collectives, body(): lax.psum(-jnp.sum(second_rowgrad[:, None] * second_soft, axis=0), ('dp',...  40.1 us
    unnamed x2, waiting for transfers between devices  35.1 us
    all_gather x1, blocking collectives, body(): lax.all_gather(router_weight, 'dp', axis=0, tiled=True)  34.5 us
    all_gather x1, blocking collectives, body(): score_full = lax.all_gather(score_grad, 'mp', axis=0, tiled=True)  7.07 us
  transfers between devices with their start and end apart: 1, of which 1 were waited for; matrix products, arithmetic and copies ran while one was open for 1% of the time, Pallas kernels for 0%

commit v1 on v0

--- a/solution.py
+++ b/solution.py
@@ -1,7 +1,14 @@
+import functools
+
 import jax
 import jax.numpy as jnp
 from jax import lax
+from jax.experimental import pallas as pl
+from jax.experimental.pallas import tpu as pltpu
 from jax.sharding import PartitionSpec as P
+
+MESH = pl.DeviceIdType.MESH
+PAIR = 2
 
 
 def neg_lse(values):
@@ -9,7 +16,7 @@
     return -(top[:, 0] + jnp.log(jnp.sum(jnp.exp(values - top), axis=1)))
 
 
-def body(hidden, router_weight, logits, first_pot, second_pot, expert_index, loss_grad):
+def plain_body(hidden, router_weight, logits, first_pot, second_pot, expert_index, loss_grad):
     experts = logits.shape[1]
     total_tokens = logits.shape[0] * lax.axis_size("dp") * lax.axis_size("mp")
     ratio = experts / total_tokens
@@ -57,6 +64,306 @@
     return (weight_grad, hidden_grad)
 
 
+def column_groups(rows, outer):
+    for group in range(1, outer + 1):
+        if outer % group == 0 and (group * PAIR * rows) % 128 == 0:
+            return group
+    return None
+
+
+def kernel(
+    devices_dp, devices_mp, ratio,
+    hidden_hbm, w_ref, logits_ref, first_ref, second_ref, index_ref, grad_ref,
+    wgrad_ref, score_ref, wfull_ref,
+    hid, part, sums, ysend, yrecv, zsend, zrecv,
+    hid_sem, w_send, w_recv, sum_send, sum_recv, score_send, score_recv,
+    y_send, y_recv, z_send, z_recv,
+):
+    outer = devices_dp // PAIR
+    total = devices_dp * devices_mp
+    rows = w_ref.shape[0]
+    tokens, experts = logits_ref.shape
+    i, m = lax.axis_index("dp"), lax.axis_index("mp")
+    me = i * devices_mp + m
+    z, y = i // PAIR, i % PAIR
+    peer = z * PAIR + 1 - y
+
+    barrier = pltpu.get_barrier_semaphore()
+
+    @pl.loop(1, total)
+    def _(d):
+        t = (me + d) % total
+        pl.semaphore_signal(
+            barrier, inc=1, device_id=(t // devices_mp, t % devices_mp), device_id_type=MESH
+        )
+
+    hid_copy = pltpu.make_async_copy(hidden_hbm, hid, hid_sem)
+    hid_copy.start()
+
+    first_exp = jnp.exp(first_ref[...])
+    second_exp = jnp.exp(second_ref[...] - first_ref[...])
+    logits = logits_ref[...]
+    e = jnp.exp(logits - jnp.max(logits, axis=1, keepdims=True))
+    q = e * first_exp
+    first_soft = e / jnp.sum(e, axis=1, keepdims=True)
+    second_soft = q / jnp.sum(q, axis=1, keepdims=True)
+    chosen = lax.broadcasted_iota(jnp.int32, (tokens, experts), 1) == index_ref[...]
+    direct = jnp.where(chosen, second_soft * second_exp * grad_ref[...], 0.0)
+    row_direct = jnp.sum(direct, axis=1, keepdims=True)
+    wfull_ref[i] = w_ref[...]
+
+    def sum_copy(slot, t, src):
+        return pltpu.make_async_remote_copy(
+            src_ref=sums.at[slot, me],
+            dst_ref=sums.at[slot, src],
+            send_sem=sum_send.at[slot, t],
+            recv_sem=sum_recv.at[slot, src],
+            device_id=(t // devices_mp, t % devices_mp),
+            device_id_type=MESH,
+        )
+
+    def start_sum(slot, value):
+        sums[slot, me] = value
+
+        @pl.loop(1, total)
+        def _(d):
+            sum_copy(slot, (me + d) % total, me).start()
+
+    def finish_sum(slot):
+        @pl.loop(1, total)
+        def _(d):
+            t = (me + d) % total
+            sum_copy(slot, t, t).wait_recv()
+
+        return jnp.sum(sums[slot], axis=0)
+
+    def w_copy(way, c, target, own=False):
+        return pltpu.make_async_remote_copy(
+            src_ref=w_ref if own else wfull_ref.at[c],
+            dst_ref=wfull_ref.at[c],
+            send_sem=w_send.at[way, c],
+            recv_sem=w_recv.at[c],
+            device_id=(target, m),
+            device_id_type=MESH,
+        )
+
+    def w_moves(step, act):
+        low, high = z - step, z + step
+        own = step == 0
+
+        @pl.when((low >= 0) & (z + 1 < outer))
+        def _():
+            act(w_copy(0, low * PAIR + y, i + PAIR, own))
+
+        @pl.when((high < outer) & (z >= 1))
+        def _():
+            act(w_copy(1, high * PAIR + y, i - PAIR, own))
+
+        @pl.when(low >= 0)
+        def _():
+            act(w_copy(2, low * PAIR + y, peer, own))
+
+        if step:
+
+            @pl.when(high < outer)
+            def _():
+                act(w_copy(2, high * PAIR + y, peer))
+
+    def w_stage(step):
+        if step:
+
+            @pl.when(z - step >= 0)
+            def _():
+                w_copy(0, (z - step) * PAIR + y, peer).wait_recv()
+
+            @pl.when(z + step < outer)
+            def _():
+                w_copy(1, (z + step) * PAIR + y, peer).wait_recv()
+
+        w_moves(step, lambda copy: copy.start())
+
+    pl.semaphore_wait(barrier, total - 1)
+    start_sum(0, jnp.sum(direct, axis=0, keepdims=True))
+    w_stage(0)
+    second_colgrad = finish_sum(0)
+    second_term = (ratio * second_exp) * second_colgrad
+    second_rowgrad = row_direct - jnp.sum(second_soft * second_term, axis=1, keepdims=True)
+    start_sum(1, -jnp.sum(second_rowgrad * second_soft, axis=0, keepdims=True))
+    if outer > 1:
+        w_stage(1)
+    rest = direct - second_soft * (second_term + second_rowgrad)
+    first_colgrad = finish_sum(1)
+    first_term = (ratio * first_exp) * first_colgrad
+    first_rowgrad = -jnp.sum(first_soft * first_term, axis=1, keepdims=True)
+    score_ref[m] = (rest - first_soft * (first_term + first_rowgrad)).astype(jnp.bfloat16)
+
+    def score_copy(t, src):
+        return pltpu.make_async_remote_copy(
+            src_ref=score_ref.at[m],
+            dst_ref=score_ref.at[src],
+            send_sem=score_send.at[t],
+            recv_sem=score_recv.at[src],
+            device_id=(i, t),
+            device_id_type=MESH,
+        )
+
+    for d in range(1, devices_mp):
+        score_copy((m + d) % devices_mp, m).start()
+    for step in range(2, outer):
+        w_stage(step)
+    hid_copy.wait()
+    for d in range(1, devices_mp):
+        t = (m + d) % devices_mp
+        score_copy(t, t).wait_recv()
+
+    score = score_ref[...].reshape(devices_mp * tokens, experts)
+    group = column_groups(rows, outer)
+    groups = outer // group
+    wide = group * PAIR * rows
+
+    def y_copy(c):
+        return pltpu.make_async_remote_copy(
+            src_ref=ysend.at[c],
+            dst_ref=yrecv.at[c],
+            send_sem=y_send.at[c],
+            recv_sem=y_recv.at[c],
+            device_id=(peer, m),
+            device_id_type=MESH,
+        )
+
+    def z_copy(c, src):
+        return pltpu.make_async_remote_copy(
+            src_ref=zsend.at[c],
+            dst_ref=zrecv.at[src],
+            send_sem=z_send.at[c],
+            recv_sem=z_recv.at[src],
+            device_id=(c * PAIR + y, m),
+            device_id_type=MESH,
+        )
+
+    def block(c, half):
+        return pl.ds(pl.multiple_of((c * PAIR + half) * rows, 16), rows)
+
+    order = [((z // group + 1 + k) % groups) for k in range(groups)]
+    for g in order:
+        columns = pl.ds(pl.multiple_of(g * wide, 128), wide)
+        part[pl.ds(pl.multiple_of(g * wide, 16), wide), :] = lax.dot_general(
+            hid[:, columns], score, (((0,), (0,)), ((), ())), preferred_element_type=jnp.float32
+        )
+        for k in range(group):
+            c = g * group + k
+            ysend[c] = part[block(c, 1 - y), :].astype(jnp.bfloat16)
+            y_copy(c).start()
+
+    for g in order:
+        for k in range(group):
+            c = g * group + k
+            y_copy(c).wait_recv()
+            both = part[block(c, y), :] + yrecv[c].astype(jnp.float32)
+
+            @pl.when(c == z)
+            def _():
+                wgrad_ref[...] = both
+
+            @pl.when(c != z)
+            def _():
+                zsend[c] = both.astype(jnp.bfloat16)
+                z_copy(c, z).start()
+
+    for c in range(outer):
+
+        @pl.when(c != z)
+        def _():
+            z_copy(c, c).wait_recv()
+            wgrad_ref[...] += zrecv[c].astype(jnp.float32)
+
+    for c in range(outer):
+        w_copy(2, c * PAIR + 1 - y, peer).wait_recv()
+
+    @pl.loop(1, total)
+    def _(d):
+        t = (me + d) % total
+        sum_copy(0, t, me).wait_send()
+        sum_copy(1, t, me).wait_send()
+
+    for step in range(outer):
+        w_moves(step, lambda copy: copy.wait_send())
+    for d in range(1, devices_mp):
+        score_copy((m + d) % devices_mp, m).wait_send()
+    for c in range(outer):
+        y_copy(c).wait_send()
+
+        @pl.when(c != z)
+        def _():
+            z_copy(c, z).wait_send()
+
+
+def kernel_body(hidden, router_weight, logits, first_pot, second_pot, expert_index, loss_grad):
+    dp, mp = lax.axis_size("dp"), lax.axis_size("mp")
+    tokens, experts = logits.shape
+    rows = router_weight.shape[0]
+    outer = dp // PAIR
+    vmem = pl.BlockSpec(memory_space=pltpu.VMEM)
+    dma = pltpu.SemaphoreType.DMA
+    weight_grad, score, weights = pl.pallas_call(
+        functools.partial(kernel, dp, mp, experts / (tokens * dp * mp)),
+        out_shape=(
+            jax.ShapeDtypeStruct((rows, experts), jnp.float32),
+            jax.ShapeDtypeStruct((mp, tokens, experts), jnp.bfloat16),
+            jax.ShapeDtypeStruct((dp, rows, experts), jnp.bfloat16),
+        ),
+        in_specs=[pl.BlockSpec(memory_space=pl.ANY)] + [vmem] * 6,
+        out_specs=(vmem, vmem, vmem),
+        scratch_shapes=[
+            pltpu.VMEM(hidden.shape, hidden.dtype),
+            pltpu.VMEM((dp * rows, experts), jnp.float32),
+            pltpu.VMEM((2, dp * mp, 1, experts), jnp.float32),
+            pltpu.VMEM((outer, rows, experts), jnp.bfloat16),
+            pltpu.VMEM((outer, rows, experts), jnp.bfloat16),
+            pltpu.VMEM((outer, rows, experts), jnp.bfloat16),
+            pltpu.VMEM((outer, rows, experts), jnp.bfloat16),
+            dma,
+            dma((3, dp)),
+            dma((dp,)),
+            dma((2, dp * mp)),
+            dma((2, dp * mp)),
+            dma((mp,)),
+            dma((mp,)),
+            dma((outer,)),
+            dma((outer,)),
+            dma((outer,)),
+            dma((outer,)),
+        ],
+        compiler_params=pltpu.CompilerParams(
+            collective_id=0, has_side_effects=True, vmem_limit_bytes=40 * 1024 * 1024
+        ),
+    )(
+        hidden,
+        router_weight,
+        logits,
+        first_pot[None, :],
+        second_pot[None, :],
+        expert_index[:, None],
+        loss_grad[:, None],
+    )
+    hidden_grad = lax.dot_general(
+        score.reshape(mp * tokens, experts),
+        weights.reshape(dp * rows, experts),
+        (((1,), (1,)), ((), ())),
+        preferred_element_type=jnp.float32,
+    ).astype(jnp.bfloat16)
+    return (weight_grad, hidden_grad)
+
+
+def body(hidden, router_weight, logits, *others):
+    dp = lax.axis_size("dp")
+    rows, tokens = router_weight.shape[0], logits.shape[0]
+    fits = dp % PAIR == 0 and rows % 16 == 0 and tokens % 16 == 0
+    if fits and column_groups(rows, dp // PAIR) is not None:
+        return kernel_body(hidden, router_weight, logits, *others)
+    return plain_body(hidden, router_weight, logits, *others)
+
+
 def solution(mesh):
     in_specs = (
         P("dp", "mp"),

time: 189 us -> 50 us (0.26)
  blocking collectives: 124 us -> 0 us
  Pallas kernels: 0 us -> 39.3 us
  waiting for transfers between devices: 35.1 us -> 0 us
  between operations: 14.1 us -> 0.67 us
  other arithmetic: 5.94 us -> 0 us
  matrix products: 6.93 us -> 2.32 us
  local copies, waits for them, and re-layouts: 2.81 us -> 7.15 us
    psum x2 -> x0, blocking collectives: 82.1 us -> none  [the longest x1 42 us: body(): second_colgrad = lax.psum(jnp.sum(direct, axis=0), ('dp', 'mp'))]
    all_gather x2 -> x0, blocking collectives: 41.6 us -> none  [the longest x1 34.5 us: body(): lax.all_gather(router_weight, 'dp', axis=0, tiled=True)]
    pallas_call x0 -> x1, Pallas kernels: none -> 39.3 us  [kernel_body(): pl.pallas_call(functools.partial(kernel, dp, mp, experts / (tokens * dp *...]
    unnamed x2 -> x0, waiting for transfers between devices: 35.1 us -> none
    dot_general x4 -> x1, matrix products: 6.93 us -> 2.32 us  [kernel_body(): lax.dot_general(score.reshape(mp * tokens, experts), weights.reshape(dp *...]
    reduce_sum x3 -> x0, other arithmetic: 3.43 us -> none  [the longest x1 1.2 us: body(): second_colgrad = lax.psum(jnp.sum(direct, axis=0), ('dp', 'mp'))]
    unnamed x5 -> x11, local copies, waits for them, and re-layouts: 2.81 us -> 5.57 us
  transfers between devices with their start and end apart: 1 -> 0, of which waited for: 1 -> 0; matrix products, arithmetic and copies ran while one was open for 1% -> 0% of each run, Pallas kernels for 0% -> 0%
where the time goes in v1:
time: 50 us; the launch traced here: 49.5 us
  Pallas kernels  39.3 us (79%)
  local copies, waits for them, and re-layouts  7.15 us (14%)
  matrix products  2.32 us (5%)
  between operations  0.67 us (1%)
    pallas_call x1, Pallas kernels, kernel_body(): pl.pallas_call(functools.partial(kernel, dp, mp, experts / (tokens * dp *...  39.3 us
    unnamed x11, local copies, waits for them, and re-layouts  5.57 us
    dot_general x1, matrix products, kernel_body(): lax.dot_general(score.reshape(mp * tokens, experts), weights.reshape(dp *...  2.32 us

profile of v1, /device:TPU:0, one launch (start us, length us, event | category | flops | bytes accessed | tf_op | source)
XLA Modules:
  0.0 49.5 jit_solution(8897592545364789524)
XLA Ops:
  0.6 0.8 %copy.9.index_ref = s32[176,1]{1,0:T(8,128)S(1)} copy(s32[176,1]{0,1:T(1,128)} %bitcast.12) | data formatting | bytes 1408 | tf_op jit(solution)/shard_map/broadcast_in_dim | solution.py:346
  1.4 0.8 %copy.10.grad_ref = f32[176,1]{1,0:T(8,128)S(1)} copy(f32[176,1]{0,1:T(1,128)} %bitcast.13) | data formatting | bytes 1408 | tf_op jit(solution)/shard_map/broadcast_in_dim | solution.py:347
  2.2 0.0 copy-start
  2.2 1.7 %copy-done = bf16[704,1792]{1,0:T(8,128)(2,1)S(1)} copy-done((bf16[704,1792]{1,0:T(8,128)(2,1)S(1)}, bf16[704,1792]{1,0:T(8,128)(2,1)}, u32[]{:S(2)}) %copy-start) | copy-done | bytes 2523160
  3.9 0.0 copy-start.1
  3.9 0.9 %copy-done.1 = f32[176,256]{1,0:T(8,128)S(1)} copy-done((f32[176,256]{1,0:T(8,128)S(1)}, f32[176,256]{1,0:T(8,128)}, u32[]{:S(2)}) %copy-start.1) | copy-done | bytes 180248
  4.9 0.0 copy-start.2
  4.9 0.9 %copy-done.2 = bf16[224,256]{1,0:T(8,128)(2,1)S(1)} copy-done((bf16[224,256]{1,0:T(8,128)(2,1)S(1)}, bf16[224,256]{1,0:T(8,128)(2,1)}, u32[]{:S(2)}) %copy-start.2) | copy-done | bytes 114712
  5.8 0.0 copy-start.3
  5.8 0.7 %copy-done.3 = f32[256]{0:T(256)S(1)} copy-done((f32[256]{0:T(256)S(1)}, f32[256]{0:T(256)}, u32[]{:S(2)}) %copy-start.3) | copy-done | bytes 1048
  6.4 0.0 copy-start.4
  6.4 0.7 %copy-done.4 = f32[256]{0:T(256)S(1)} copy-done((f32[256]{0:T(256)S(1)}, f32[256]{0:T(256)}, u32[]{:S(2)}) %copy-start.4) | copy-done | bytes 1048
  7.1 39.3 %shard_map.86 = (f32[224,256]{1,0:T(8,128)S(1)}, bf16[4,176,256]{2,1,0:T(8,128)(2,1)S(1)}, bf16[8,224,256]{2,1,0:T(8,128)(2,1)S(1)}) custom-call(bf16[704,1792]{1,0:T(8,128)(2,1)S(1)} %copy-done, bf16[224,256]{1,0:T(8,128)(2,1)S(1)} %copy-done.2, f32[176,256]{1,0:T(8,128)S(1)} %copy-done.1, f32[1,256]{1,0:T(1,128)S(1)} %bitcast.10, f32[1,256]{1,0:T(1,128)S(1)} %bitcast.11, ...), custom_call_target="tpu_custom_call" | custom-call | tf_op jit(solution)/shard_map/pallas_call | solution.py:308
  46.5 2.3 %convolution_convert_fusion = bf16[704,1792]{1,0:T(8,128)(2,1)} fusion(bf16[704,256]{1,0:T(8,128)(2,1)S(1)} %bitcast.9, bf16[1792,256]{1,0:T(8,128)(2,1)S(1)} %bitcast.8), kind=kOutput, calls=%fused_computation | convolution fusion | flops 647184384 | bytes 3801088 | tf_op jit(solution)/shard_map/dot_general | solution.py:349
  48.8 0.7 %copy.12 = f32[224,256]{1,0:T(8,128)} copy(f32[224,256]{1,0:T(8,128)S(1)} %get-tuple-element.10) | data formatting | bytes 458752
Async XLA Ops:
  2.2 1.7 %copy-start = (bf16[704,1792]{1,0:T(8,128)(2,1)S(1)}, bf16[704,1792]{1,0:T(8,128)(2,1)}, u32[]{:S(2)}) copy-start(bf16[704,1792]{1,0:T(8,128)(2,1)} %hidden_hbm.1) | copy-start | bytes 7569412
  3.9 0.9 %copy-start.1 = (f32[176,256]{1,0:T(8,128)S(1)}, f32[176,256]{1,0:T(8,128)}, u32[]{:S(2)}) copy-start(f32[176,256]{1,0:T(8,128)} %logits_ref.1) | copy-start | bytes 540676
  4.9 0.9 %copy-start.2 = (bf16[224,256]{1,0:T(8,128)(2,1)S(1)}, bf16[224,256]{1,0:T(8,128)(2,1)}, u32[]{:S(2)}) copy-start(bf16[224,256]{1,0:T(8,128)(2,1)} %w_ref.1) | copy-start | bytes 344068
  5.8 0.7 %copy-start.3 = (f32[256]{0:T(256)S(1)}, f32[256]{0:T(256)}, u32[]{:S(2)}) copy-start(f32[256]{0:T(256)} %param.10) | copy-start | bytes 3076
  6.4 0.7 %copy-start.4 = (f32[256]{0:T(256)S(1)}, f32[256]{0:T(256)}, u32[]{:S(2)}) copy-start(f32[256]{0:T(256)} %param.11) | copy-start | bytes 3076

commit v2 on v1

--- a/solution.py
+++ b/solution.py
@@ -8,6 +8,7 @@
 from jax.sharding import PartitionSpec as P
 
 MESH = pl.DeviceIdType.MESH
+BITS = [1 << k for k in range(12)]
 PAIR = 2
 
 
@@ -64,25 +65,19 @@
     return (weight_grad, hidden_grad)
 
 
-def column_groups(rows, outer):
-    for group in range(1, outer + 1):
-        if outer % group == 0 and (group * PAIR * rows) % 128 == 0:
-            return group
-    return None
-
-
 def kernel(
     devices_dp, devices_mp, ratio,
     hidden_hbm, w_ref, logits_ref, first_ref, second_ref, index_ref, grad_ref,
     wgrad_ref, score_ref, wfull_ref,
-    hid, part, sums, ysend, yrecv, zsend, zrecv,
-    hid_sem, w_send, w_recv, sum_send, sum_recv, score_send, score_recv,
+    hid, turned, logits, index, grad, pots, soft, part, sums, ysend, yrecv, zsend, zrecv,
+    in_sem, w_send, w_recv, sum_send, sum_recv, row_send, row_recv,
     y_send, y_recv, z_send, z_recv,
 ):
     outer = devices_dp // PAIR
     total = devices_dp * devices_mp
     rows = w_ref.shape[0]
     tokens, experts = logits_ref.shape
+    half = devices_mp // PAIR
     i, m = lax.axis_index("dp"), lax.axis_index("mp")
     me = i * devices_mp + m
     z, y = i // PAIR, i % PAIR
@@ -97,20 +92,51 @@
             barrier, inc=1, device_id=(t // devices_mp, t % devices_mp), device_id_type=MESH
         )
 
-    hid_copy = pltpu.make_async_copy(hidden_hbm, hid, hid_sem)
-    hid_copy.start()
-
-    first_exp = jnp.exp(first_ref[...])
-    second_exp = jnp.exp(second_ref[...] - first_ref[...])
-    logits = logits_ref[...]
-    e = jnp.exp(logits - jnp.max(logits, axis=1, keepdims=True))
-    q = e * first_exp
-    first_soft = e / jnp.sum(e, axis=1, keepdims=True)
-    second_soft = q / jnp.sum(q, axis=1, keepdims=True)
-    chosen = lax.broadcasted_iota(jnp.int32, (tokens, experts), 1) == index_ref[...]
-    direct = jnp.where(chosen, second_soft * second_exp * grad_ref[...], 0.0)
+    inputs = [
+        (logits_ref, logits.at[m]),
+        (index_ref, index.at[m]),
+        (grad_ref, grad.at[m]),
+        (first_ref, pots.at[0]),
+        (second_ref, pots.at[1]),
+        (w_ref, wfull_ref.at[i]),
+        (hidden_hbm, hid),
+    ]
+    loads = [pltpu.make_async_copy(src, dst, in_sem.at[k]) for k, (src, dst) in enumerate(inputs)]
+    for load in loads:
+        load.start()
+    for load in loads[:-1]:
+        load.wait()
+
+    first_exp = jnp.exp(pots[0])
+    second_exp = jnp.exp(pots[1] - pots[0])
+
+    def soften(b):
+        scores = logits[b]
+        e = jnp.exp(scores - jnp.max(scores, axis=1, keepdims=True))
+        q = e * first_exp
+        second_soft = q / jnp.sum(q, axis=1, keepdims=True)
+        chosen = lax.broadcasted_iota(jnp.int32, (tokens, experts), 1) == index[b].T
+        soft[0, b] = e / jnp.sum(e, axis=1, keepdims=True)
+        soft[1, b] = second_soft
+        soft[2, b] = jnp.where(chosen, second_soft * second_exp * grad[b].T, 0.0)
+
+    def row_copy(kind, src, t):
+        ref = (logits, index, grad)[kind]
+        return pltpu.make_async_remote_copy(
+            src_ref=ref.at[src],
+            dst_ref=ref.at[src],
+            send_sem=row_send.at[kind, src, t],
+            recv_sem=row_recv.at[kind, src],
+            device_id=(i, t),
+            device_id_type=MESH,
+        )
+
+    beside = (m // PAIR) * PAIR + 1 - m % PAIR
+    same = [(m + PAIR * d) % devices_mp for d in range(1, half)]
+
+    soften(m)
+    direct = soft[2, m]
     row_direct = jnp.sum(direct, axis=1, keepdims=True)
-    wfull_ref[i] = w_ref[...]
 
     def sum_copy(slot, t, src):
         return pltpu.make_async_remote_copy(
@@ -137,9 +163,9 @@
 
         return jnp.sum(sums[slot], axis=0)
 
-    def w_copy(way, c, target, own=False):
+    def w_copy(way, c, target):
         return pltpu.make_async_remote_copy(
-            src_ref=w_ref if own else wfull_ref.at[c],
+            src_ref=wfull_ref.at[c],
             dst_ref=wfull_ref.at[c],
             send_sem=w_send.at[way, c],
             recv_sem=w_recv.at[c],
@@ -147,21 +173,23 @@
             device_id_type=MESH,
         )
 
-    def w_moves(step, act):
+    def w_along(step, act):
         low, high = z - step, z + step
-        own = step == 0
 
         @pl.when((low >= 0) & (z + 1 < outer))
         def _():
-            act(w_copy(0, low * PAIR + y, i + PAIR, own))
+            act(w_copy(0, low * PAIR + y, i + PAIR))
 
         @pl.when((high < outer) & (z >= 1))
         def _():
-            act(w_copy(1, high * PAIR + y, i - PAIR, own))
+            act(w_copy(1, high * PAIR + y, i - PAIR))
+
+    def w_across(step, act):
+        low, high = z - step, z + step
 
         @pl.when(low >= 0)
         def _():
-            act(w_copy(2, low * PAIR + y, peer, own))
+            act(w_copy(2, low * PAIR + y, peer))
 
         if step:
 
@@ -180,46 +208,49 @@
             def _():
                 w_copy(1, (z + step) * PAIR + y, peer).wait_recv()
 
-        w_moves(step, lambda copy: copy.start())
+        w_along(step, lambda copy: copy.start())
+        w_across(step, lambda copy: copy.start())
 
     pl.semaphore_wait(barrier, total - 1)
     start_sum(0, jnp.sum(direct, axis=0, keepdims=True))
+    for t in [beside] + same:
+        for kind in range(3):
+            row_copy(kind, m, t).start()
     w_stage(0)
+    loads[-1].wait()
+    cut = hid.shape[1] // 2
+    turned[:cut, :] = hid[:, :cut].T
     second_colgrad = finish_sum(0)
     second_term = (ratio * second_exp) * second_colgrad
+    second_soft = soft[1, m]
     second_rowgrad = row_direct - jnp.sum(second_soft * second_term, axis=1, keepdims=True)
     start_sum(1, -jnp.sum(second_rowgrad * second_soft, axis=0, keepdims=True))
+    for t in same:
+        for kind in range(3):
+            row_copy(kind, t, beside).wait_recv()
+            row_copy(kind, t, beside).start()
     if outer > 1:
         w_stage(1)
-    rest = direct - second_soft * (second_term + second_rowgrad)
+    turned[cut:, :] = hid[:, cut:].T
+    for t in same:
+        soften(t)
+    for t in [beside] + [(t // PAIR) * PAIR + 1 - t % PAIR for t in same]:
+        for kind in range(3):
+            row_copy(kind, t, beside).wait_recv()
+        soften(t)
     first_colgrad = finish_sum(1)
     first_term = (ratio * first_exp) * first_colgrad
-    first_rowgrad = -jnp.sum(first_soft * first_term, axis=1, keepdims=True)
-    score_ref[m] = (rest - first_soft * (first_term + first_rowgrad)).astype(jnp.bfloat16)
-
-    def score_copy(t, src):
-        return pltpu.make_async_remote_copy(
-            src_ref=score_ref.at[m],
-            dst_ref=score_ref.at[src],
-            send_sem=score_send.at[t],
-            recv_sem=score_recv.at[src],
-            device_id=(i, t),
-            device_id_type=MESH,
-        )
-
-    for d in range(1, devices_mp):
-        score_copy((m + d) % devices_mp, m).start()
-    for step in range(2, outer):
-        w_stage(step)
-    hid_copy.wait()
-    for d in range(1, devices_mp):
-        t = (m + d) % devices_mp
-        score_copy(t, t).wait_recv()
+    for b in range(devices_mp):
+        first_soft, second_soft, direct = soft[0, b], soft[1, b], soft[2, b]
+        second_rowgrad = jnp.sum(direct - second_soft * second_term, axis=1, keepdims=True)
+        first_rowgrad = -jnp.sum(first_soft * first_term, axis=1, keepdims=True)
+        score_ref[b] = (
+            direct
+            - second_soft * (second_term + second_rowgrad)
+            - first_soft * (first_term + first_rowgrad)
+        ).astype(jnp.bfloat16)
 
     score = score_ref[...].reshape(devices_mp * tokens, experts)
-    group = column_groups(rows, outer)
-    groups = outer // group
-    wide = group * PAIR * rows
 
     def y_copy(c):
         return pltpu.make_async_remote_copy(
@@ -244,31 +275,28 @@
     def block(c, half):
         return pl.ds(pl.multiple_of((c * PAIR + half) * rows, 16), rows)
 
-    order = [((z // group + 1 + k) % groups) for k in range(groups)]
-    for g in order:
-        columns = pl.ds(pl.multiple_of(g * wide, 128), wide)
-        part[pl.ds(pl.multiple_of(g * wide, 16), wide), :] = lax.dot_general(
-            hid[:, columns], score, (((0,), (0,)), ((), ())), preferred_element_type=jnp.float32
-        )
-        for k in range(group):
-            c = g * group + k
-            ysend[c] = part[block(c, 1 - y), :].astype(jnp.bfloat16)
-            y_copy(c).start()
-
-    for g in order:
-        for k in range(group):
-            c = g * group + k
-            y_copy(c).wait_recv()
-            both = part[block(c, y), :] + yrecv[c].astype(jnp.float32)
-
-            @pl.when(c == z)
-            def _():
-                wgrad_ref[...] = both
-
-            @pl.when(c != z)
-            def _():
-                zsend[c] = both.astype(jnp.bfloat16)
-                z_copy(c, z).start()
+    def product(c, side):
+        return jnp.dot(turned[block(c, side), :], score, preferred_element_type=jnp.float32)
+
+    if outer & (outer - 1) == 0:
+        order = [z + sum(bit * (1 - 2 * (z // bit % 2)) for bit in BITS if flip & bit) for flip in range(outer - 1, -1, -1)]
+    else:
+        order = [(z + 1 + k) % outer for k in range(outer)]
+    for c in order:
+        ysend[c] = product(c, 1 - y).astype(jnp.bfloat16)
+        y_copy(c).start()
+    for step in range(2, outer - 1):
+        w_stage(step)
+    for c in order:
+        part[c] = product(c, y)
+    for c in order[:-1]:
+        y_copy(c).wait_recv()
+        zsend[c] = (part[c] + yrecv[c].astype(jnp.float32)).astype(jnp.bfloat16)
+        z_copy(c, z).start()
+    if outer > 2:
+        w_stage(outer - 1)
+    y_copy(z).wait_recv()
+    wgrad_ref[...] = part[z] + yrecv[z].astype(jnp.float32)
 
     for c in range(outer):
 
@@ -287,9 +315,13 @@
         sum_copy(1, t, me).wait_send()
 
     for step in range(outer):
-        w_moves(step, lambda copy: copy.wait_send())
-    for d in range(1, devices_mp):
-        score_copy((m + d) % devices_mp, m).wait_send()
+        w_along(step, lambda copy: copy.wait_send())
+        w_across(step, lambda copy: copy.wait_send())
+    for kind in range(3):
+        for t in [beside] + same:
+            row_copy(kind, m, t).wait_send()
+        for t in same:
+            row_copy(kind, t, beside).wait_send()
     for c in range(outer):
         y_copy(c).wait_send()
 
@@ -312,30 +344,36 @@
             jax.ShapeDtypeStruct((mp, tokens, experts), jnp.bfloat16),
             jax.ShapeDtypeStruct((dp, rows, experts), jnp.bfloat16),
         ),
-        in_specs=[pl.BlockSpec(memory_space=pl.ANY)] + [vmem] * 6,
+        in_specs=[pl.BlockSpec(memory_space=pltpu.HBM)] * 7,
         out_specs=(vmem, vmem, vmem),
         scratch_shapes=[
             pltpu.VMEM(hidden.shape, hidden.dtype),
-            pltpu.VMEM((dp * rows, experts), jnp.float32),
+            pltpu.VMEM(hidden.shape[::-1], hidden.dtype),
+            pltpu.VMEM((mp, tokens, experts), jnp.float32),
+            pltpu.VMEM((mp, 1, tokens), jnp.int32),
+            pltpu.VMEM((mp, 1, tokens), jnp.float32),
+            pltpu.VMEM((2, 1, experts), jnp.float32),
+            pltpu.VMEM((3, mp, tokens, experts), jnp.float32),
+            pltpu.VMEM((outer, rows, experts), jnp.float32),
             pltpu.VMEM((2, dp * mp, 1, experts), jnp.float32),
             pltpu.VMEM((outer, rows, experts), jnp.bfloat16),
             pltpu.VMEM((outer, rows, experts), jnp.bfloat16),
             pltpu.VMEM((outer, rows, experts), jnp.bfloat16),
             pltpu.VMEM((outer, rows, experts), jnp.bfloat16),
-            dma,
+            dma((7,)),
             dma((3, dp)),
             dma((dp,)),
             dma((2, dp * mp)),
             dma((2, dp * mp)),
-            dma((mp,)),
-            dma((mp,)),
+            dma((3, mp, mp)),
+            dma((3, mp)),
             dma((outer,)),
             dma((outer,)),
             dma((outer,)),
             dma((outer,)),
         ],
         compiler_params=pltpu.CompilerParams(
-            collective_id=0, has_side_effects=True, vmem_limit_bytes=40 * 1024 * 1024
+            collective_id=0, has_side_effects=True, vmem_limit_bytes=67043328
         ),
     )(
         hidden,
@@ -343,8 +381,8 @@
         logits,
         first_pot[None, :],
         second_pot[None, :],
-        expert_index[:, None],
-        loss_grad[:, None],
+        expert_index[None, :],
+        loss_grad[None, :],
     )
     hidden_grad = lax.dot_general(
         score.reshape(mp * tokens, experts),
@@ -358,8 +396,7 @@
 def body(hidden, router_weight, logits, *others):
     dp = lax.axis_size("dp")
     rows, tokens = router_weight.shape[0], logits.shape[0]
-    fits = dp % PAIR == 0 and rows % 16 == 0 and tokens % 16 == 0
-    if fits and column_groups(rows, dp // PAIR) is not None:
+    if dp % PAIR == 0 and lax.axis_size("mp") % PAIR == 0 and rows % 16 == 0 and tokens % 16 == 0:
         return kernel_body(hidden, router_weight, logits, *others)
     return plain_body(hidden, router_weight, logits, *others)
 

time: 50 us -> 42.8 us (0.86)
  local copies, waits for them, and re-layouts: 7.15 us -> 0.69 us
  Pallas kernels: 39.3 us -> 37.6 us
  matrix products: 2.32 us -> 3.65 us
    unnamed x11 -> x3, local copies, waits for them, and re-layouts: 5.57 us -> 0.69 us
    pallas_call x1, Pallas kernels: 39.3 us -> 37.6 us  [kernel_body(): pl.pallas_call(functools.partial(kernel, dp, mp, experts / (tokens * dp *...]
    broadcast_in_dim x2 -> x0, local copies, waits for them, and re-layouts: 1.57 us -> none  [the longest x1 0.79 us: kernel_body(): loss_grad[:, None]]
    dot_general x1, matrix products: 2.32 us -> 3.65 us  [kernel_body(): lax.dot_general(score.reshape(mp * tokens, experts), weights.reshape(dp *...]
where the time goes in v2:
time: 42.8 us; the launch traced here: 42.6 us
  Pallas kernels  37.6 us (88%)
  matrix products  3.65 us (9%)
  local copies, waits for them, and re-layouts  0.69 us (2%)
  between operations  0.65 us (2%)
    pallas_call x1, Pallas kernels, kernel_body(): pl.pallas_call(functools.partial(kernel, dp, mp, experts / (tokens * dp *...  37.6 us
    dot_general x1, matrix products, kernel_body(): lax.dot_general(score.reshape(mp * tokens, experts), weights.reshape(dp *...  3.65 us

profile of v2, /device:TPU:0, one launch (start us, length us, event | category | flops | bytes accessed | tf_op | source)
XLA Modules:
  0.0 42.6 jit_solution(4706897783551092917)
XLA Ops:
  0.6 37.6 %shard_map.86 = (f32[224,256]{1,0:T(8,128)}, bf16[4,176,256]{2,1,0:T(8,128)(2,1)}, bf16[8,224,256]{2,1,0:T(8,128)(2,1)}) custom-call(bf16[704,1792]{1,0:T(8,128)(2,1)} %hidden_hbm.1, bf16[224,256]{1,0:T(8,128)(2,1)} %w_ref.1, f32[176,256]{1,0:T(8,128)} %logits_ref.1, f32[1,256]{1,0:T(1,128)} %bitcast.10, f32[1,256]{1,0:T(1,128)} %bitcast.11, ...), custom_call_target="tpu_custom_call" | custom-call | tf_op jit(solution)/shard_map/pallas_call | solution.py:340
  38.3 0.0 copy-start
  38.3 3.6 %convolution_convert_fusion = bf16[704,1792]{1,0:T(8,128)(2,1)} fusion(bf16[704,256]{1,0:T(8,128)(2,1)} %bitcast.9, bf16[1792,256]{1,0:T(8,128)(2,1)} %bitcast.8), kind=kOutput, calls=%fused_computation | convolution fusion | flops 647184384 | bytes 3801088 | tf_op jit(solution)/shard_map/dot_general | solution.py:387
  41.9 0.0 copy-done
  41.9 0.7 %copy.10 = f32[224,256]{1,0:T(8,128)} copy(f32[224,256]{1,0:T(8,128)S(1)} %copy-done) | data formatting | bytes 458752
Async XLA Ops:
  38.3 3.7 %copy-start = (f32[224,256]{1,0:T(8,128)S(1)}, f32[224,256]{1,0:T(8,128)}, u32[]{:S(2)}) copy-start(f32[224,256]{1,0:T(8,128)} %get-tuple-element.10) | copy-start | bytes 688132

commit v3 on v2

--- a/solution.py
+++ b/solution.py
@@ -65,13 +65,20 @@
     return (weight_grad, hidden_grad)
 
 
+def column_groups(rows, outer):
+    for group in range(1, outer + 1):
+        if outer % group == 0 and (group * PAIR * rows) % 128 == 0:
+            return group
+    return None
+
+
 def kernel(
     devices_dp, devices_mp, ratio,
     hidden_hbm, w_ref, logits_ref, first_ref, second_ref, index_ref, grad_ref,
-    wgrad_ref, score_ref, wfull_ref,
-    hid, turned, logits, index, grad, pots, soft, part, sums, ysend, yrecv, zsend, zrecv,
+    wgrad_out, hgrad_out,
+    wgrad_ref, hgrad, score_ref, wfull_ref, hid, turned, logits, index, grad, pots, soft, part, sums, ysend, yrecv, zsend, zrecv,
     in_sem, w_send, w_recv, sum_send, sum_recv, row_send, row_recv,
-    y_send, y_recv, z_send, z_recv,
+    y_send, y_recv, z_send, z_recv, out_sem,
 ):
     outer = devices_dp // PAIR
     total = devices_dp * devices_mp
@@ -289,6 +296,27 @@
         w_stage(step)
     for c in order:
         part[c] = product(c, y)
+
+    group = column_groups(rows, outer)
+    groups, wide = outer // group, group * PAIR * rows
+
+    def hidden_out(g):
+        columns = pl.ds(pl.multiple_of(g * wide, 128), wide)
+        return pltpu.make_async_copy(
+            hgrad.at[:, columns], hgrad_out.at[:, columns], out_sem.at[g]
+        )
+
+    def hidden_part(g):
+        for k in range(group):
+            w_copy(2, (g * group + k) * PAIR + 1 - y, peer).wait_recv()
+        weights = wfull_ref[pl.ds(g * group * PAIR, group * PAIR)].reshape(wide, experts)
+        hgrad[:, pl.ds(pl.multiple_of(g * wide, 128), wide)] = lax.dot_general(
+            score, weights, (((1,), (1,)), ((), ())), preferred_element_type=jnp.float32
+        ).astype(jnp.bfloat16)
+        hidden_out(g).start()
+
+    if groups > 1:
+        hidden_part(z // group)
     for c in order[:-1]:
         y_copy(c).wait_recv()
         zsend[c] = (part[c] + yrecv[c].astype(jnp.float32)).astype(jnp.bfloat16)
@@ -305,8 +333,10 @@
             z_copy(c, c).wait_recv()
             wgrad_ref[...] += zrecv[c].astype(jnp.float32)
 
-    for c in range(outer):
-        w_copy(2, c * PAIR + 1 - y, peer).wait_recv()
+    wgrad_copy = pltpu.make_async_copy(wgrad_ref, wgrad_out, out_sem.at[groups])
+    wgrad_copy.start()
+    for k in range(1, groups) if groups > 1 else [0]:
+        hidden_part((z // group + k) % groups)
 
     @pl.loop(1, total)
     def _(d):
@@ -329,24 +359,32 @@
         def _():
             z_copy(c, z).wait_send()
 
+    wgrad_copy.wait()
+    for g in range(groups):
+        hidden_out(g).wait()
+
 
 def kernel_body(hidden, router_weight, logits, first_pot, second_pot, expert_index, loss_grad):
     dp, mp = lax.axis_size("dp"), lax.axis_size("mp")
     tokens, experts = logits.shape
     rows = router_weight.shape[0]
     outer = dp // PAIR
-    vmem = pl.BlockSpec(memory_space=pltpu.VMEM)
+    hbm = pl.BlockSpec(memory_space=pltpu.HBM)
+    group = column_groups(rows, outer)
     dma = pltpu.SemaphoreType.DMA
-    weight_grad, score, weights = pl.pallas_call(
+    return pl.pallas_call(
         functools.partial(kernel, dp, mp, experts / (tokens * dp * mp)),
         out_shape=(
             jax.ShapeDtypeStruct((rows, experts), jnp.float32),
-            jax.ShapeDtypeStruct((mp, tokens, experts), jnp.bfloat16),
-            jax.ShapeDtypeStruct((dp, rows, experts), jnp.bfloat16),
+            jax.ShapeDtypeStruct((mp * tokens, dp * rows), jnp.bfloat16),
         ),
-        in_specs=[pl.BlockSpec(memory_space=pltpu.HBM)] * 7,
-        out_specs=(vmem, vmem, vmem),
+        in_specs=[hbm] * 7,
+        out_specs=(hbm, hbm),
         scratch_shapes=[
+            pltpu.VMEM((rows, experts), jnp.float32),
+            pltpu.VMEM(hidden.shape, hidden.dtype),
+            pltpu.VMEM((mp, tokens, experts), jnp.bfloat16),
+            pltpu.VMEM((dp, rows, experts), jnp.bfloat16),
             pltpu.VMEM(hidden.shape, hidden.dtype),
             pltpu.VMEM(hidden.shape[::-1], hidden.dtype),
             pltpu.VMEM((mp, tokens, experts), jnp.float32),
@@ -371,6 +409,7 @@
             dma((outer,)),
             dma((outer,)),
             dma((outer,)),
+            dma((outer // group + 1,)),
         ],
         compiler_params=pltpu.CompilerParams(
             collective_id=0, has_side_effects=True, vmem_limit_bytes=67043328
@@ -384,19 +423,13 @@
         expert_index[None, :],
         loss_grad[None, :],
     )
-    hidden_grad = lax.dot_general(
-        score.reshape(mp * tokens, experts),
-        weights.reshape(dp * rows, experts),
-        (((1,), (1,)), ((), ())),
-        preferred_element_type=jnp.float32,
-    ).astype(jnp.bfloat16)
-    return (weight_grad, hidden_grad)
 
 
 def body(hidden, router_weight, logits, *others):
     dp = lax.axis_size("dp")
     rows, tokens = router_weight.shape[0], logits.shape[0]
-    if dp % PAIR == 0 and lax.axis_size("mp") % PAIR == 0 and rows % 16 == 0 and tokens % 16 == 0:
+    pairs = dp % PAIR == 0 and lax.axis_size("mp") % PAIR == 0
+    if pairs and rows % 16 == 0 and tokens % 16 == 0 and column_groups(rows, dp // PAIR):
         return kernel_body(hidden, router_weight, logits, *others)
     return plain_body(hidden, router_weight, logits, *others)
 

time: 42.8 us -> 43.4 us (1.014)
  local copies, waits for them, and re-layouts: 0.69 us -> 4.97 us
  matrix products: 3.65 us -> 0 us
    unnamed x3 -> x2, local copies, waits for them, and re-layouts: 0.69 us -> 4.97 us
    dot_general x1 -> x0, matrix products: 3.65 us -> none  [kernel_body(): lax.dot_general(score.reshape(mp * tokens, experts), weights.reshape(dp *...]
where the time goes in v3:
time: 43.4 us; the launch traced here: 43.2 us
  Pallas kernels  37.6 us (87%)
  local copies, waits for them, and re-layouts  4.97 us (11%)
  between operations  0.64 us (1%)
    pallas_call x1, Pallas kernels, kernel_body(): pl.pallas_call(functools.partial(kernel, dp, mp, experts / (tokens * dp *...  37.6 us
    unnamed x2, local copies, waits for them, and re-layouts  4.97 us

profile of v3, /device:TPU:0, one launch (start us, length us, event | category | flops | bytes accessed | tf_op | source)
XLA Modules:
  0.0 43.2 jit_solution(15178887558341536037)
XLA Ops:
  0.6 37.6 %shard_map.86 = (f32[224,256]{1,0:T(8,128)}, bf16[704,1792]{1,0:T(8,128)(2,1)}) custom-call(bf16[704,1792]{1,0:T(8,128)(2,1)} %hidden_hbm.1, bf16[224,256]{1,0:T(8,128)(2,1)} %w_ref.1, f32[176,256]{1,0:T(8,128)} %logits_ref.1, f32[1,256]{1,0:T(1,128)} %bitcast.4, f32[1,256]{1,0:T(1,128)} %bitcast.5, s32[1,176]{1,0:T(1,128)} %bitcast.6, f32[1,176]{1,0:T(1,128)} %bitcast.7), custom_call_target="tpu_custom_call" | custom-call | tf_op jit(solution)/shard_map/pallas_call | solution.py:375
  38.3 1.6 %copy.11 = f32[224,256]{1,0:T(8,128)} copy(f32[224,256]{1,0:T(8,128)} %get-tuple-element.4) | data formatting | bytes 458752
  39.9 3.3 %copy.12 = bf16[704,1792]{1,0:T(8,128)(2,1)} copy(bf16[704,1792]{1,0:T(8,128)(2,1)} %get-tuple-element.5) | data formatting | bytes 5046272

commit v4 on v2

--- a/solution.py
+++ b/solution.py
@@ -68,10 +68,10 @@
 def kernel(
     devices_dp, devices_mp, ratio,
     hidden_hbm, w_ref, logits_ref, first_ref, second_ref, index_ref, grad_ref,
-    wgrad_ref, score_ref, wfull_ref,
-    hid, turned, logits, index, grad, pots, soft, part, sums, ysend, yrecv, zsend, zrecv,
+    wgrad_out, score_out, wfull_out,
+    wgrad_ref, score_ref, wfull_ref, hid, turned, logits, index, grad, pots, soft, part, sums, ysend, yrecv, zsend, zrecv,
     in_sem, w_send, w_recv, sum_send, sum_recv, row_send, row_recv,
-    y_send, y_recv, z_send, z_recv,
+    y_send, y_recv, z_send, z_recv, out_sem,
 ):
     outer = devices_dp // PAIR
     total = devices_dp * devices_mp
@@ -289,6 +289,23 @@
         w_stage(step)
     for c in order:
         part[c] = product(c, y)
+
+    group = 2 if outer % 2 == 0 else 1
+    groups = outer // group
+    score_copy = pltpu.make_async_copy(score_ref, score_out, out_sem.at[groups + 1])
+    score_copy.start()
+
+    def rows_out(g):
+        chunks = pl.ds(g * group * PAIR, group * PAIR)
+        return pltpu.make_async_copy(wfull_ref.at[chunks], wfull_out.at[chunks], out_sem.at[g])
+
+    def rows_ready(g):
+        for k in range(group):
+            w_copy(2, (g * group + k) * PAIR + 1 - y, peer).wait_recv()
+        rows_out(g).start()
+
+    if groups > 1:
+        rows_ready(z // group)
     for c in order[:-1]:
         y_copy(c).wait_recv()
         zsend[c] = (part[c] + yrecv[c].astype(jnp.float32)).astype(jnp.bfloat16)
@@ -305,8 +322,10 @@
             z_copy(c, c).wait_recv()
             wgrad_ref[...] += zrecv[c].astype(jnp.float32)
 
-    for c in range(outer):
-        w_copy(2, c * PAIR + 1 - y, peer).wait_recv()
+    wgrad_copy = pltpu.make_async_copy(wgrad_ref, wgrad_out, out_sem.at[groups])
+    wgrad_copy.start()
+    for k in range(1, groups) if groups > 1 else [0]:
+        rows_ready((z // group + k) % groups)
 
     @pl.loop(1, total)
     def _(d):
@@ -329,13 +348,18 @@
         def _():
             z_copy(c, z).wait_send()
 
+    wgrad_copy.wait()
+    score_copy.wait()
+    for g in range(groups):
+        rows_out(g).wait()
+
 
 def kernel_body(hidden, router_weight, logits, first_pot, second_pot, expert_index, loss_grad):
     dp, mp = lax.axis_size("dp"), lax.axis_size("mp")
     tokens, experts = logits.shape
     rows = router_weight.shape[0]
     outer = dp // PAIR
-    vmem = pl.BlockSpec(memory_space=pltpu.VMEM)
+    hbm = pl.BlockSpec(memory_space=pltpu.HBM)
     dma = pltpu.SemaphoreType.DMA
     weight_grad, score, weights = pl.pallas_call(
         functools.partial(kernel, dp, mp, experts / (tokens * dp * mp)),
@@ -344,9 +368,12 @@
             jax.ShapeDtypeStruct((mp, tokens, experts), jnp.bfloat16),
             jax.ShapeDtypeStruct((dp, rows, experts), jnp.bfloat16),
         ),
-        in_specs=[pl.BlockSpec(memory_space=pltpu.HBM)] * 7,
-        out_specs=(vmem, vmem, vmem),
+        in_specs=[hbm] * 7,
+        out_specs=(hbm, hbm, hbm),
         scratch_shapes=[
+            pltpu.VMEM((rows, experts), jnp.float32),
+            pltpu.VMEM((mp, tokens, experts), jnp.bfloat16),
+            pltpu.VMEM((dp, rows, experts), jnp.bfloat16),
             pltpu.VMEM(hidden.shape, hidden.dtype),
             pltpu.VMEM(hidden.shape[::-1], hidden.dtype),
             pltpu.VMEM((mp, tokens, experts), jnp.float32),
@@ -371,6 +398,7 @@
             dma((outer,)),
             dma((outer,)),
             dma((outer,)),
+            dma((outer + 2,)),
         ],
         compiler_params=pltpu.CompilerParams(
             collective_id=0, has_side_effects=True, vmem_limit_bytes=67043328
@@ -396,7 +424,8 @@
 def body(hidden, router_weight, logits, *others):
     dp = lax.axis_size("dp")
     rows, tokens = router_weight.shape[0], logits.shape[0]
-    if dp % PAIR == 0 and lax.axis_size("mp") % PAIR == 0 and rows % 16 == 0 and tokens % 16 == 0:
+    pairs = dp % PAIR == 0 and lax.axis_size("mp") % PAIR == 0
+    if pairs and rows % 16 == 0 and tokens % 16 == 0:
         return kernel_body(hidden, router_weight, logits, *others)
     return plain_body(hidden, router_weight, logits, *others)
 

time: 42.8 us -> 42 us (0.981)
  Pallas kernels: 37.6 us -> 36.9 us
    pallas_call x1, Pallas kernels: 37.6 us -> 36.9 us  [kernel_body(): pl.pallas_call(functools.partial(kernel, dp, mp, experts / (tokens * dp *...]
where the time goes in v4:
time: 42 us; the launch traced here: 41.9 us
  Pallas kernels  36.9 us (88%)
  matrix products  3.64 us (9%)
  local copies, waits for them, and re-layouts  0.69 us (2%)
  between operations  0.65 us (2%)
    pallas_call x1, Pallas kernels, kernel_body(): pl.pallas_call(functools.partial(kernel, dp, mp, experts / (tokens * dp *...  36.9 us
    dot_general x1, matrix products, kernel_body(): lax.dot_general(score.reshape(mp * tokens, experts), weights.reshape(dp *...  3.64 us

profile of v4, /device:TPU:0, one launch (start us, length us, event | category | flops | bytes accessed | tf_op | source)
XLA Modules:
  0.0 41.9 jit_solution(12757636080467868355)
XLA Ops:
  0.6 36.9 %shard_map.86 = (f32[224,256]{1,0:T(8,128)}, bf16[4,176,256]{2,1,0:T(8,128)(2,1)}, bf16[8,224,256]{2,1,0:T(8,128)(2,1)}) custom-call(bf16[704,1792]{1,0:T(8,128)(2,1)} %hidden_hbm.1, bf16[224,256]{1,0:T(8,128)(2,1)} %w_ref.1, f32[176,256]{1,0:T(8,128)} %logits_ref.1, f32[1,256]{1,0:T(1,128)} %bitcast.10, f32[1,256]{1,0:T(1,128)} %bitcast.11, ...), custom_call_target="tpu_custom_call" | custom-call | tf_op jit(solution)/shard_map/pallas_call | solution.py:364
  37.5 0.0 copy-start
  37.5 3.6 %convolution_convert_fusion = bf16[704,1792]{1,0:T(8,128)(2,1)} fusion(bf16[704,256]{1,0:T(8,128)(2,1)} %bitcast.9, bf16[1792,256]{1,0:T(8,128)(2,1)} %bitcast.8), kind=kOutput, calls=%fused_computation | convolution fusion | flops 647184384 | bytes 3801088 | tf_op jit(solution)/shard_map/dot_general | solution.py:415
  41.2 0.0 copy-done
  41.2 0.7 %copy.10 = f32[224,256]{1,0:T(8,128)} copy(f32[224,256]{1,0:T(8,128)S(1)} %copy-done) | data formatting | bytes 458752
Async XLA Ops:
  37.5 3.7 %copy-start = (f32[224,256]{1,0:T(8,128)S(1)}, f32[224,256]{1,0:T(8,128)}, u32[]{:S(2)}) copy-start(f32[224,256]{1,0:T(8,128)} %get-tuple-element.10) | copy-start | bytes 688132
